TPU v7x, 32 devices: a whole 2x2x4 slice. The times are simulated.
32 devices in a mesh: rows: 8 (over y, x, core), hub: 4 (over z).
Axes of the slice: x: 2, y: 2, z: 4, core: 2. Of those that a mesh axis runs over, the one named last changes fastest.
Arguments:
- tail_blocks: float32 [2304, 128, 128], P(('rows', 'hub')), may hold values from -0.21875 to 0.21875
- tail_row: int32 [2304], P(('rows', 'hub')), may hold values from 0 to 15
- tail_owner: int32 [2304, 1], P(('rows', 'hub')), may hold values from 0 to 7; in each aligned block of 72 rows (0 to 71, 72 to 143, ...) at most 27 rows name the same one
- tail_slot: int32 [2304], P(('rows', 'hub')), may hold values from 0 to 63
- hub_blocks: float32 [768, 128, 128], P(('rows', 'hub')), may hold values from -0.21875 to 0.21875
- hub_row: int32 [768], P(('rows', 'hub')), may hold values from 0 to 15
- hub_col: int32 [768], P(('rows', 'hub')), may hold values from 0 to 127
- x_tail: float32 [2048, 128], P(('rows', 'hub')), may hold values from 0 to 0.5
- cost_tail: float32 [2048, 128], P(('rows', 'hub')), may hold values from -6 to 6
- upper_tail: float32 [2048, 128], P(('rows', 'hub')), may hold values from 0.5 to 2
- x_hub: float32 [128, 128], P('hub'), may hold values from 0 to 0.5
- cost_hub: float32 [128, 128], P('hub'), may hold values from -6 to 6
- upper_hub: float32 [128, 128], P('hub'), may hold values from 0.5 to 2
- duals: float32 [512, 128], P(('rows', 'hub')), may hold values from 0 to 1
- demand: float32 [512, 128], P(('rows', 'hub')), may hold values from -6 to 6
Outputs:
- x_tail_out: float32 [2048, 128], P(('rows', 'hub'))
- x_hub_out: float32 [128, 128], P('hub')
- duals_out: float32 [512, 128], P(('rows', 'hub'))
Inputs may be any that keep to these rules, and one draw needn't show every extreme that they name: `tail_owner`: among the blocks of one device no owner is named more than 27 times; on some device one owner is named exactly 27 times.
All inputs are finite; a program needn't handle non-finite values.
Results may differ from a plain program's by a relative error of at most 0.0001.
Values sent between devices are 32-bit elements; how exact they have to be, the bound alone decides.
No kernel may reach another device: no remote copies, remote signals or barrier semaphores. Data moves between devices by JAX's collectives and lax.ppermute only.
A program may use at most 64 MiB of HBM per device.

v0:
```python
import jax
import jax.numpy as jnp
from jax import lax
from jax.sharding import PartitionSpec as P

ITERS = 3
primal_step = 0.25
dual_step = 0.25


def on_device(
    tail_blocks,
    tail_row,
    tail_owner,
    tail_slot,
    hub_blocks,
    hub_row,
    hub_col,
    x_tail,
    cost_tail,
    upper_tail,
    x_hub,
    cost_hub,
    upper_hub,
    duals,
    demand,
):
    highest = lax.Precision.HIGHEST
    row_devs = lax.axis_size("rows")
    hub_devs = lax.axis_size("hub")
    tail_count = tail_blocks.shape[0]
    col_blocks = x_tail.shape[0]
    row_blocks = duals.shape[0]
    hub_share = x_hub.shape[0]
    hub_total = hub_share * hub_devs
    width = x_tail.shape[1]
    capacity = max(2, 3 * tail_count // row_devs)
    owners = tail_owner[:, 0]
    hits = (owners[:, None] == jnp.arange(row_devs, dtype=jnp.int32)[None, :]).astype(jnp.int32)
    within = jnp.sum(jnp.cumsum(hits, axis=0) * hits, axis=1) - 1
    places = owners * capacity + within
    asked_slots = jnp.zeros((row_devs * capacity,), jnp.int32).at[places].set(tail_slot)
    requested = lax.all_to_all(
        asked_slots.reshape(row_devs, capacity), "rows", split_axis=0, concat_axis=0, tiled=True
    ).reshape(-1)
    collector = (jnp.arange(col_blocks, dtype=jnp.int32)[:, None] == requested[None, :]).astype(
        jnp.float32
    )
    tail_rowpick = (jnp.arange(row_blocks, dtype=jnp.int32)[:, None] == tail_row[None, :]).astype(
        jnp.float32
    )
    hub_rowpick = (jnp.arange(row_blocks, dtype=jnp.int32)[:, None] == hub_row[None, :]).astype(
        jnp.float32
    )
    hub_state = x_hub
    hub_pick = (jnp.arange(hub_total, dtype=jnp.int32)[:, None] == hub_col[None, :]).astype(
        jnp.float32
    )
    tail_state = x_tail
    for iteration in range(ITERS):
        tail_terms = jnp.einsum("bij,bi->bj", tail_blocks, duals[tail_row], precision=highest)
        outgoing = jnp.zeros((row_devs * capacity, width), jnp.float32).at[places].set(tail_terms)
        arrived = lax.all_to_all(
            outgoing.reshape(row_devs, capacity, width),
            "rows",
            split_axis=0,
            concat_axis=0,
            tiled=True,
        )
        tail_image = jnp.dot(
            collector,
            arrived.reshape(-1, width),
            precision=highest,
            preferred_element_type=jnp.float32,
        )
        tail_next = jnp.minimum(
            jnp.maximum(tail_state - primal_step * (cost_tail - tail_image), 0.0), upper_tail
        )
        tail_extra = 2.0 * tail_next - tail_state
        hub_terms = jnp.einsum("bij,bi->bj", hub_blocks, duals[hub_row], precision=highest)
        hub_partial = jnp.dot(
            hub_pick, hub_terms, precision=highest, preferred_element_type=jnp.float32
        )
        hub_sums = lax.psum_scatter(hub_partial, "hub", scatter_dimension=0, tiled=True)
        hub_sums = lax.psum(hub_sums, "rows")
        hub_next = jnp.minimum(
            jnp.maximum(hub_state - primal_step * (cost_hub - hub_sums), 0.0), upper_hub
        )
        hub_extra = 2.0 * hub_next - hub_state
        hub_full = lax.all_gather(hub_extra, "hub", axis=0, tiled=True)
        gathered = lax.all_gather(tail_extra, "rows", axis=0, tiled=True)
        tail_picked = gathered[owners * col_blocks + tail_slot]
        tail_product = jnp.einsum("bij,bj->bi", tail_blocks, tail_picked, precision=highest)
        hub_product = jnp.einsum("bij,bj->bi", hub_blocks, hub_full[hub_col], precision=highest)
        primal_image = jnp.dot(
            tail_rowpick, tail_product, precision=highest, preferred_element_type=jnp.float32
        )
        primal_image = primal_image + jnp.dot(
            hub_rowpick, hub_product, precision=highest, preferred_element_type=jnp.float32
        )
        duals = jnp.maximum(duals + dual_step * (demand - primal_image), 0.0)
        tail_state = tail_next
        hub_state = hub_next
    return (tail_state, hub_state, duals)


def solution(mesh):
    in_specs = (
        P(("rows", "hub"), None, None),
        P(("rows", "hub")),
        P(("rows", "hub"), None),
        P(("rows", "hub")),
        P(("rows", "hub"), None, None),
        P(("rows", "hub")),
        P(("rows", "hub")),
        P(("rows", "hub"), None),
        P(("rows", "hub"), None),
        P(("rows", "hub"), None),
        P("hub", None),
        P("hub", None),
        P("hub", None),
        P(("rows", "hub"), None),
        P(("rows", "hub"), None),
    )
    out_specs = (P(("rows", "hub"), None), P("hub", None), P(("rows", "hub"), None))
    return jax.shard_map(
        on_device, mesh=mesh, in_specs=in_specs, out_specs=out_specs, check_vma=False
    )
```

profile of v0, /device:TPU:0, one launch (start us, length us, event | category | flops | bytes accessed | tf_op | source)
XLA Modules:
  0.0 261.1 jit_solution(8980955782605521598)
XLA Ops:
  11.3 5.2 %all-to-all-start = ((s32[8,1,27]{2,1,0:T(1,128)}), s32[8,1,27]{2,1,0:T(1,128)S(1)}, u32[]{:S(2)}, u32[]{:S(2)}) async-start(s32[8,1,27]{2,1,0:T(1,128)} %all_to_all.15), calls=%async_computation | async-start | bytes 8192 | tf_op jit(solution)/shard_map/all_to_all | solution.py:43
  24.7 5.8 %fusion.52 = f32[72,1,128]{2,1,0:T(1,128)S(1)} fusion(f32[72,128,1]{1,2,0:T(1,128)S(1)} %bitcast.112, f32[72,128,128]{2,1,0:T(8,128)} %param.15), kind=kOutput, calls=%fused_computation.99 | convolution fusion | flops 14155776 | bytes 4792320 | tf_op jit(solution)/shard_map/bij,bi->bj/dot_general | solution.py:61
  32.0 4.2 %all-to-all-start.1 = ((f32[8,27,128]{2,1,0:T(8,128)}), f32[8,27,128]{2,1,0:T(8,128)S(1)}, u32[]{:S(2)}, u32[]{:S(2)}) async-start(f32[8,27,128]{2,1,0:T(8,128)} %reshape.42), calls=%async_computation.1 | async-start | bytes 262144 | tf_op jit(solution)/shard_map/all_to_all | solution.py:63
  37.4 4.2 %all-to-all-done.1 = f32[8,27,128]{2,1,0:T(8,128)S(1)} async-done(((f32[8,27,128]{2,1,0:T(8,128)}), f32[8,27,128]{2,1,0:T(8,128)S(1)}, u32[]{:S(2)}, u32[]{:S(2)}) %all-to-all-start.1) | async-done | bytes 110624 | tf_op jit(solution)/shard_map/all_to_all | solution.py:63
  41.9 8.4 %all_gather.18 = f32[512,128]{1,0:T(8,128)S(1)} all-gather(f32[64,128]{1,0:T(8,128)S(1)} %get-tuple-element.9), channel_id=1, replica_groups=mesh['rows'=8,'hub'=4] {'rows'}, dimensions={0}, use_global_device_ids=true | all-gather | bytes 294912 | tf_op jit(solution)/shard_map/all_gather | solution.py:91
  50.9 9.2 %fusion.53 = f32[72,1,128]{2,1,0:T(1,128)S(1)} fusion(f32[72,128,1]{1,2,0:T(1,128)S(1)} %bitcast.109, f32[72,128,128]{2,1,0:T(8,128)} %param.15), kind=kOutput, calls=%fused_computation.100 | convolution fusion | flops 14155776 | bytes 4792320 | tf_op jit(solution)/shard_map/bij,bj->bi/dot_general | solution.py:93
  60.2 23.7 %psum.21 = f32[32,128]{1,0:T(8,128)S(1)} all-reduce(f32[32,128]{1,0:T(8,128)} %reduce-scatter.4.cloned.1.call-done), channel_id=1, replica_groups=mesh['rows'=8,'hub'=4] {'rows'}, use_global_device_ids=true, to_apply=%region_5.6 | all-reduce | flops 4096 | bytes 32768 | tf_op jit(solution)/shard_map/psum | solution.py:85
  84.0 13.6 %all_gather.19 = f32[128,128]{1,0:T(8,128)S(1)} all-gather(f32[32,128]{1,0:T(8,128)S(1)} %get-tuple-element.7), channel_id=1, replica_groups=mesh['rows'=8,'hub'=4] {'hub'}, dimensions={0}, use_global_device_ids=true | all-gather | bytes 81920 | tf_op jit(solution)/shard_map/all_gather | solution.py:90
  102.0 5.8 %fusion.56 = f32[72,1,128]{2,1,0:T(1,128)S(1)} fusion(f32[72,128,1]{1,2,0:T(1,128)S(1)} %bitcast.110, f32[72,128,128]{2,1,0:T(8,128)} %param.15), kind=kOutput, calls=%fused_computation.103 | convolution fusion | flops 14155776 | bytes 4792320 | tf_op jit(solution)/shard_map/bij,bi->bj/dot_general | solution.py:61
  109.2 3.4 %all-to-all-start.2 = ((f32[8,27,128]{2,1,0:T(8,128)}), f32[8,27,128]{2,1,0:T(8,128)S(1)}, u32[]{:S(2)}, u32[]{:S(2)}) async-start(f32[8,27,128]{2,1,0:T(8,128)} %reshape.44), calls=%async_computation.3 | async-start | bytes 262144 | tf_op jit(solution)/shard_map/all_to_all | solution.py:63
  115.0 3.2 %all-to-all-done.2 = f32[8,27,128]{2,1,0:T(8,128)S(1)} async-done(((f32[8,27,128]{2,1,0:T(8,128)}), f32[8,27,128]{2,1,0:T(8,128)S(1)}, u32[]{:S(2)}, u32[]{:S(2)}) %all-to-all-start.2) | async-done | bytes 110624 | tf_op jit(solution)/shard_map/all_to_all | solution.py:63
  118.4 8.4 %all_gather.20 = f32[512,128]{1,0:T(8,128)S(1)} all-gather(f32[64,128]{1,0:T(8,128)S(1)} %get-tuple-element.11), channel_id=1, replica_groups=mesh['rows'=8,'hub'=4] {'rows'}, dimensions={0}, use_global_device_ids=true | all-gather | bytes 294912 | tf_op jit(solution)/shard_map/all_gather | solution.py:91
  127.3 9.2 %fusion.57 = f32[72,1,128]{2,1,0:T(1,128)S(1)} fusion(f32[72,128,1]{1,2,0:T(1,128)S(1)} %bitcast.111, f32[72,128,128]{2,1,0:T(8,128)} %param.15), kind=kOutput, calls=%fused_computation.104 | convolution fusion | flops 14155776 | bytes 4792320 | tf_op jit(solution)/shard_map/bij,bj->bi/dot_general | solution.py:93
  136.7 23.6 %psum.22 = f32[32,128]{1,0:T(8,128)S(1)} all-reduce(f32[32,128]{1,0:T(8,128)} %reduce-scatter.6.cloned.1.call-done), channel_id=1, replica_groups=mesh['rows'=8,'hub'=4] {'rows'}, use_global_device_ids=true, to_apply=%region_8.9 | all-reduce | flops 4096 | bytes 32768 | tf_op jit(solution)/shard_map/psum | solution.py:85
  160.3 13.4 %all_gather.21 = f32[128,128]{1,0:T(8,128)S(1)} all-gather(f32[32,128]{1,0:T(8,128)S(1)} %get-tuple-element.5), channel_id=1, replica_groups=mesh['rows'=8,'hub'=4] {'hub'}, dimensions={0}, use_global_device_ids=true | all-gather | bytes 81920 | tf_op jit(solution)/shard_map/all_gather | solution.py:90
  174.2 2.5 fusion.59
  178.1 5.8 %fusion.60 = f32[72,1,128]{2,1,0:T(1,128)S(1)} fusion(f32[72,128,1]{1,2,0:T(1,128)S(1)} %bitcast.107, f32[72,128,128]{2,1,0:T(8,128)} %param.15), kind=kOutput, calls=%fused_computation.107 | convolution fusion | flops 14155776 | bytes 4792320 | tf_op jit(solution)/shard_map/bij,bi->bj/dot_general | solution.py:61
  185.3 3.4 %all-to-all-start.3 = ((f32[8,27,128]{2,1,0:T(8,128)}), f32[8,27,128]{2,1,0:T(8,128)S(1)}, u32[]{:S(2)}, u32[]{:S(2)}) async-start(f32[8,27,128]{2,1,0:T(8,128)} %reshape.46), calls=%async_computation.5 | async-start | bytes 262144 | tf_op jit(solution)/shard_map/all_to_all | solution.py:63
  191.0 3.2 %all-to-all-done.3 = f32[8,27,128]{2,1,0:T(8,128)S(1)} async-done(((f32[8,27,128]{2,1,0:T(8,128)}), f32[8,27,128]{2,1,0:T(8,128)S(1)}, u32[]{:S(2)}, u32[]{:S(2)}) %all-to-all-start.3) | async-done | bytes 110624 | tf_op jit(solution)/shard_map/all_to_all | solution.py:63
  195.1 8.3 %all_gather.22 = f32[512,128]{1,0:T(8,128)S(1)} all-gather(f32[64,128]{1,0:T(8,128)S(1)} %get-tuple-element.13), channel_id=1, replica_groups=mesh['rows'=8,'hub'=4] {'rows'}, dimensions={0}, use_global_device_ids=true | all-gather | bytes 294912 | tf_op jit(solution)/shard_map/all_gather | solution.py:91
  204.0 9.2 %fusion.62 = f32[72,1,128]{2,1,0:T(1,128)S(1)} fusion(f32[72,128,1]{1,2,0:T(1,128)S(1)} %bitcast.108, f32[72,128,128]{2,1,0:T(8,128)} %param.15), kind=kOutput, calls=%fused_computation.109 | convolution fusion | flops 14155776 | bytes 4792320 | tf_op jit(solution)/shard_map/bij,bj->bi/dot_general | solution.py:93
  213.3 23.6 %psum.23 = f32[32,128]{1,0:T(8,128)S(1)} all-reduce(f32[32,128]{1,0:T(8,128)} %reduce-scatter.8.cloned.1.call-done), channel_id=1, replica_groups=mesh['rows'=8,'hub'=4] {'rows'}, use_global_device_ids=true, to_apply=%region_11.12 | all-reduce | flops 4096 | bytes 32768 | tf_op jit(solution)/shard_map/psum | solution.py:85
  237.6 13.1 %all_gather.23 = f32[128,128]{1,0:T(8,128)S(1)} all-gather(f32[32,128]{1,0:T(8,128)S(1)} %get-tuple-element.3), channel_id=1, replica_groups=mesh['rows'=8,'hub'=4] {'hub'}, dimensions={0}, use_global_device_ids=true | all-gather | bytes 81920 | tf_op jit(solution)/shard_map/all_gather | solution.py:90
  251.2 2.5 fusion.63
  (91 shorter events, 34.1 us)
Async XLA Ops:
  7.2 11.3 %copy-start = (f32[24,128,128]{2,1,0:T(8,128)S(1)}, f32[24,128,128]{2,1,0:T(8,128)}, u32[]{:S(2)}) copy-start(f32[24,128,128]{2,1,0:T(8,128)} %param.19) | copy-start | bytes 4718596
  7.2 34.5 %copy-start.7 = (f32[64,128]{1,0:T(8,128)S(1)}, f32[64,128]{1,0:T(8,128)}, u32[]{:S(2)}) copy-start(f32[64,128]{1,0:T(8,128)} %param.22) | copy-start | bytes 98308
  7.2 34.5 %copy-start.3 = (f32[64,128]{1,0:T(8,128)S(1)}, f32[64,128]{1,0:T(8,128)}, u32[]{:S(2)}) copy-start(f32[64,128]{1,0:T(8,128)} %param.23) | copy-start | bytes 98308
  7.2 34.5 %copy-start.2 = (f32[64,128]{1,0:T(8,128)S(1)}, f32[64,128]{1,0:T(8,128)}, u32[]{:S(2)}) copy-start(f32[64,128]{1,0:T(8,128)} %param.24) | copy-start | bytes 98308
  11.3 20.7 %all-to-all-start = ((s32[8,1,27]{2,1,0:T(1,128)}), s32[8,1,27]{2,1,0:T(1,128)S(1)}, u32[]{:S(2)}, u32[]{:S(2)}) async-start(s32[8,1,27]{2,1,0:T(1,128)} %all_to_all.15), calls=%async_computation | async-start | bytes 8192 | tf_op jit(solution)/shard_map/all_to_all | solution.py:43
  16.5 43.7 %reduce-scatter.4.cloned.1.call-start = ((), (), s32[]{:S(2)}) async-start(), calls=%async_computation.7 | async-start | bytes 81920 | tf_op jit(solution)/shard_map/reduce_scatter | solution.py:84
  24.7 35.4 %copy-start.10 = (s32[72]{0:T(128)S(1)}, s32[72]{0:T(128)}, u32[]{:S(2)}) copy-start(s32[72]{0:T(128)} %param.16) | copy-start | bytes 868
  24.7 59.2 %copy-start.4 = (f32[32,128]{1,0:T(8,128)S(1)}, f32[32,128]{1,0:T(8,128)}, u32[]{:S(2)}) copy-start(f32[32,128]{1,0:T(8,128)} %param.27) | copy-start | bytes 49156
  24.7 59.2 %copy-start.5 = (f32[32,128]{1,0:T(8,128)S(1)}, f32[32,128]{1,0:T(8,128)}, u32[]{:S(2)}) copy-start(f32[32,128]{1,0:T(8,128)} %param.26) | copy-start | bytes 49156
  24.7 59.2 %copy-start.8 = (f32[32,128]{1,0:T(8,128)S(1)}, f32[32,128]{1,0:T(8,128)}, u32[]{:S(2)}) copy-start(f32[32,128]{1,0:T(8,128)} %param.25) | copy-start | bytes 49156
  30.5 70.1 %copy-start.1 = (f32[16,128]{1,0:T(8,128)S(1)}, f32[16,128]{1,0:T(8,128)}, u32[]{:S(2)}) copy-start(f32[16,128]{1,0:T(8,128)} %param.28) | copy-start | bytes 24580
  30.5 70.1 %copy-start.6 = (f32[16,128]{1,0:T(8,128)S(1)}, f32[16,128]{1,0:T(8,128)}, u32[]{:S(2)}) copy-start(f32[16,128]{1,0:T(8,128)} %param.29) | copy-start | bytes 24580
  30.5 70.2 %copy-start.11 = (s32[24]{0:T(128)S(1)}, s32[24]{0:T(128)}, u32[]{:S(2)}) copy-start(s32[24]{0:T(128)} %param.20) | copy-start | bytes 292
  32.0 9.7 %all-to-all-start.1 = ((f32[8,27,128]{2,1,0:T(8,128)}), f32[8,27,128]{2,1,0:T(8,128)S(1)}, u32[]{:S(2)}, u32[]{:S(2)}) async-start(f32[8,27,128]{2,1,0:T(8,128)} %reshape.42), calls=%async_computation.1 | async-start | bytes 262144 | tf_op jit(solution)/shard_map/all_to_all | solution.py:63
  60.2 53.9 %copy-start.9 = (s32[24]{0:T(128)S(1)}, s32[24]{0:T(128)}, u32[]{:S(2)}) copy-start(s32[24]{0:T(128)} %param.21) | copy-start | bytes 292
  109.2 8.9 %all-to-all-start.2 = ((f32[8,27,128]{2,1,0:T(8,128)}), f32[8,27,128]{2,1,0:T(8,128)S(1)}, u32[]{:S(2)}, u32[]{:S(2)}) async-start(f32[8,27,128]{2,1,0:T(8,128)} %reshape.44), calls=%async_computation.3 | async-start | bytes 262144 | tf_op jit(solution)/shard_map/all_to_all | solution.py:63
  112.7 24.0 %reduce-scatter.6.cloned.1.call-start = ((), (), s32[]{:S(2)}) async-start(), calls=%async_computation.8 | async-start | bytes 81920 | tf_op jit(solution)/shard_map/reduce_scatter | solution.py:84
  185.3 8.9 %all-to-all-start.3 = ((f32[8,27,128]{2,1,0:T(8,128)}), f32[8,27,128]{2,1,0:T(8,128)S(1)}, u32[]{:S(2)}, u32[]{:S(2)}) async-start(f32[8,27,128]{2,1,0:T(8,128)} %reshape.46), calls=%async_computation.5 | async-start | bytes 262144 | tf_op jit(solution)/shard_map/all_to_all | solution.py:63
  188.7 24.6 %reduce-scatter.8.cloned.1.call-start = ((), (), s32[]{:S(2)}) async-start(), calls=%async_computation.9 | async-start | bytes 81920 | tf_op jit(solution)/shard_map/reduce_scatter | solution.py:84
Sparse Core Ops, SparseCore 0:
  21.5 20.9 reduce-scatter.3
  115.7 20.7 reduce-scatter.5
  191.8 20.7 reduce-scatter.7
where the time goes:
time: 262 us; the launch traced here: 261 us
  blocking collectives  136 us (52%)
  matrix products  62.6 us (24%)
  starting transfers between devices  16.3 us (6%)
  local copies, waits for them, and re-layouts  15 us (6%)
  between operations  14 us (5%)
  waiting for transfers between devices  10.7 us (4%)
  other arithmetic  6.44 us (2%)
    psum x3, blocking collectives, on_device(): hub_sums = lax.psum(hub_sums, 'rows')  70.9 us
    all_gather x3, blocking collectives, on_device(): hub_full = lax.all_gather(hub_extra, 'hub', axis=0, tiled=True)  40.1 us
    dot_general x3, matrix products, on_device(): jnp.einsum('bij,bj->bi', tail_blocks, tail_picked, precision=highest)  27.6 us
    all_gather x3, blocking collectives, on_device(): gathered = lax.all_gather(tail_extra, 'rows', axis=0, tiled=True)  25 us
    dot_general x3, matrix products, on_device(): jnp.einsum('bij,bi->bj', tail_blocks, duals[tail_row], precision=highest)  17.4 us
    all_to_all x3, starting transfers between devices, on_device(): lax.all_to_all(outgoing.reshape(row_devs, capacity, width), 'rows', split...  11 us
    all_to_all x3, waiting for transfers between devices, on_device(): lax.all_to_all(outgoing.reshape(row_devs, capacity, width), 'rows', split...  10.6 us
    dot_general x3, matrix products, on_device(): jnp.einsum('bij,bj->bi', hub_blocks, hub_full[hub_col], precision=highest)  7.63 us
  transfers between devices with their start and end apart: 7, of which 3 were waited for; matrix products, arithmetic and copies ran while one was open for 20% of the time, Pallas kernels for 0%

commit v1 on v0

--- a/solution.py
+++ b/solution.py
@@ -82,7 +82,7 @@
             hub_pick, hub_terms, precision=highest, preferred_element_type=jnp.float32
         )
         hub_sums = lax.psum_scatter(hub_partial, "hub", scatter_dimension=0, tiled=True)
-        hub_sums = lax.psum(hub_sums, "rows")
+        hub_sums = jnp.sum(lax.all_gather(hub_sums, "rows"), 0)
         hub_next = jnp.minimum(
             jnp.maximum(hub_state - primal_step * (cost_hub - hub_sums), 0.0), upper_hub
         )

time: 262 us -> 220 us (0.84)
  blocking collectives: 136 us -> 92.7 us
    psum x3 -> x0, blocking collectives: 70.9 us -> none  [on_device(): hub_sums = lax.psum(hub_sums, 'rows')]
    all_gather x0 -> x3, blocking collectives: none -> 27.6 us  [on_device(): hub_sums = jnp.sum(lax.all_gather(hub_sums, 'rows'), 0)]
  transfers between devices with their start and end apart: 7 -> 7, of which waited for: 3 -> 3; matrix products, arithmetic and copies ran while one was open for 20% -> 23% of each run, Pallas kernels for 0% -> 0%
where the time goes in v1:
time: 220 us; the launch traced here: 219 us
  blocking collectives  92.7 us (42%)
  matrix products  62.6 us (28%)
  starting transfers between devices  16.2 us (7%)
  local copies, waits for them, and re-layouts  15 us (7%)
  between operations  14 us (6%)
  waiting for transfers between devices  12 us (5%)
  other arithmetic  6.48 us (3%)
    all_gather x3, blocking collectives, on_device(): hub_full = lax.all_gather(hub_extra, 'hub', axis=0, tiled=True)  40 us
    all_gather x3, blocking collectives, on_device(): hub_sums = jnp.sum(lax.all_gather(hub_sums, 'rows'), 0)  27.6 us
    dot_general x3, matrix products, on_device(): jnp.einsum('bij,bj->bi', tail_blocks, tail_picked, precision=highest)  27.6 us
    all_gather x3, blocking collectives, on_device(): gathered = lax.all_gather(tail_extra, 'rows', axis=0, tiled=True)  25 us
    dot_general x3, matrix products, on_device(): jnp.einsum('bij,bi->bj', tail_blocks, duals[tail_row], precision=highest)  17.4 us
    all_to_all x3, waiting for transfers between devices, on_device(): lax.all_to_all(outgoing.reshape(row_devs, capacity, width), 'rows', split...  11.9 us
    all_to_all x3, starting transfers between devices, on_device(): lax.all_to_all(outgoing.reshape(row_devs, capacity, width), 'rows', split...  10.9 us
    dot_general x3, matrix products, on_device(): jnp.einsum('bij,bj->bi', hub_blocks, hub_full[hub_col], precision=highest)  7.63 us
  transfers between devices with their start and end apart: 7, of which 3 were waited for; matrix products, arithmetic and copies ran while one was open for 23% of the time, Pallas kernels for 0%

profile of v1, /device:TPU:0, one launch (start us, length us, event | category | flops | bytes accessed | tf_op | source)
XLA Modules:
  0.0 219.0 jit_solution(322656416827709993)
XLA Ops:
  11.3 5.2 %all-to-all-start = ((s32[8,1,27]{2,1,0:T(1,128)}), s32[8,1,27]{2,1,0:T(1,128)S(1)}, u32[]{:S(2)}, u32[]{:S(2)}) async-start(s32[8,1,27]{2,1,0:T(1,128)} %all_to_all.15), calls=%async_computation | async-start | bytes 8192 | tf_op jit(solution)/shard_map/all_to_all | solution.py:43
  24.7 5.8 %fusion.52 = f32[72,1,128]{2,1,0:T(1,128)S(1)} fusion(f32[72,128,1]{1,2,0:T(1,128)S(1)} %bitcast.118, f32[72,128,128]{2,1,0:T(8,128)} %param.15), kind=kOutput, calls=%fused_computation.99 | convolution fusion | flops 14155776 | bytes 4792320 | tf_op jit(solution)/shard_map/bij,bi->bj/dot_general | solution.py:61
  32.0 4.2 %all-to-all-start.1 = ((f32[8,27,128]{2,1,0:T(8,128)}), f32[8,27,128]{2,1,0:T(8,128)S(1)}, u32[]{:S(2)}, u32[]{:S(2)}) async-start(f32[8,27,128]{2,1,0:T(8,128)} %reshape.42), calls=%async_computation.1 | async-start | bytes 262144 | tf_op jit(solution)/shard_map/all_to_all | solution.py:63
  37.4 4.2 %all-to-all-done.1 = f32[8,27,128]{2,1,0:T(8,128)S(1)} async-done(((f32[8,27,128]{2,1,0:T(8,128)}), f32[8,27,128]{2,1,0:T(8,128)S(1)}, u32[]{:S(2)}, u32[]{:S(2)}) %all-to-all-start.1) | async-done | bytes 110624 | tf_op jit(solution)/shard_map/all_to_all | solution.py:63
  41.9 8.4 %all_gather.36 = f32[512,128]{1,0:T(8,128)S(1)} all-gather(f32[64,128]{1,0:T(8,128)S(1)} %get-tuple-element.9), channel_id=1, replica_groups=mesh['rows'=8,'hub'=4] {'rows'}, dimensions={0}, use_global_device_ids=true | all-gather | bytes 294912 | tf_op jit(solution)/shard_map/all_gather | solution.py:91
  50.9 9.2 %fusion.53 = f32[72,1,128]{2,1,0:T(1,128)S(1)} fusion(f32[72,128,1]{1,2,0:T(1,128)S(1)} %bitcast.115, f32[72,128,128]{2,1,0:T(8,128)} %param.15), kind=kOutput, calls=%fused_computation.100 | convolution fusion | flops 14155776 | bytes 4792320 | tf_op jit(solution)/shard_map/bij,bj->bi/dot_general | solution.py:93
  60.2 9.2 %all-gather = f32[256,128]{1,0:T(8,128)S(1)} all-gather(f32[32,128]{1,0:T(8,128)} %reduce-scatter.4.cloned.1.call-done), channel_id=2, replica_groups=mesh['rows'=8,'hub'=4] {'rows'}, dimensions={0}, use_global_device_ids=true | all-gather | bytes 147456 | tf_op jit(solution)/shard_map/all_gather | solution.py:85
  69.4 13.5 %all_gather.39 = f32[128,128]{1,0:T(8,128)S(1)} all-gather(f32[32,128]{1,0:T(8,128)S(1)} %get-tuple-element.7), channel_id=1, replica_groups=mesh['rows'=8,'hub'=4] {'hub'}, dimensions={0}, use_global_device_ids=true | all-gather | bytes 81920 | tf_op jit(solution)/shard_map/all_gather | solution.py:90
  87.4 5.8 %fusion.56 = f32[72,1,128]{2,1,0:T(1,128)S(1)} fusion(f32[72,128,1]{1,2,0:T(1,128)S(1)} %bitcast.116, f32[72,128,128]{2,1,0:T(8,128)} %param.15), kind=kOutput, calls=%fused_computation.103 | convolution fusion | flops 14155776 | bytes 4792320 | tf_op jit(solution)/shard_map/bij,bi->bj/dot_general | solution.py:61
  94.6 3.4 %all-to-all-start.2 = ((f32[8,27,128]{2,1,0:T(8,128)}), f32[8,27,128]{2,1,0:T(8,128)S(1)}, u32[]{:S(2)}, u32[]{:S(2)}) async-start(f32[8,27,128]{2,1,0:T(8,128)} %reshape.44), calls=%async_computation.3 | async-start | bytes 262144 | tf_op jit(solution)/shard_map/all_to_all | solution.py:63
  100.3 3.1 %all-to-all-done.2 = f32[8,27,128]{2,1,0:T(8,128)S(1)} async-done(((f32[8,27,128]{2,1,0:T(8,128)}), f32[8,27,128]{2,1,0:T(8,128)S(1)}, u32[]{:S(2)}, u32[]{:S(2)}) %all-to-all-start.2) | async-done | bytes 110624 | tf_op jit(solution)/shard_map/all_to_all | solution.py:63
  103.7 8.3 %all_gather.40 = f32[512,128]{1,0:T(8,128)S(1)} all-gather(f32[64,128]{1,0:T(8,128)S(1)} %get-tuple-element.11), channel_id=1, replica_groups=mesh['rows'=8,'hub'=4] {'rows'}, dimensions={0}, use_global_device_ids=true | all-gather | bytes 294912 | tf_op jit(solution)/shard_map/all_gather | solution.py:91
  112.6 9.2 %fusion.57 = f32[72,1,128]{2,1,0:T(1,128)S(1)} fusion(f32[72,128,1]{1,2,0:T(1,128)S(1)} %bitcast.117, f32[72,128,128]{2,1,0:T(8,128)} %param.15), kind=kOutput, calls=%fused_computation.104 | convolution fusion | flops 14155776 | bytes 4792320 | tf_op jit(solution)/shard_map/bij,bj->bi/dot_general | solution.py:93
  122.0 9.3 %all-gather.1 = f32[256,128]{1,0:T(8,128)S(1)} all-gather(f32[32,128]{1,0:T(8,128)} %reduce-scatter.6.cloned.1.call-done), channel_id=3, replica_groups=mesh['rows'=8,'hub'=4] {'rows'}, dimensions={0}, use_global_device_ids=true | all-gather | bytes 147456 | tf_op jit(solution)/shard_map/all_gather | solution.py:85
  131.3 13.4 %all_gather.43 = f32[128,128]{1,0:T(8,128)S(1)} all-gather(f32[32,128]{1,0:T(8,128)S(1)} %get-tuple-element.5), channel_id=1, replica_groups=mesh['rows'=8,'hub'=4] {'hub'}, dimensions={0}, use_global_device_ids=true | all-gather | bytes 81920 | tf_op jit(solution)/shard_map/all_gather | solution.py:90
  145.2 2.5 %fusion.59 = f32[24,1,128]{2,1,0:T(1,128)S(1)} fusion(f32[24,128,1]{1,2,0:T(1,128)S(1)} %bitcast.126, f32[24,128,128]{2,1,0:T(8,128)S(1)} %copy-done), kind=kOutput, calls=%fused_computation.106 | convolution fusion | flops 4718592 | bytes 1597440 | tf_op jit(solution)/shard_map/bij,bj->bi/dot_general | solution.py:94
  150.5 5.8 %fusion.60 = f32[72,1,128]{2,1,0:T(1,128)S(1)} fusion(f32[72,128,1]{1,2,0:T(1,128)S(1)} %bitcast.113, f32[72,128,128]{2,1,0:T(8,128)} %param.15), kind=kOutput, calls=%fused_computation.107 | convolution fusion | flops 14155776 | bytes 4792320 | tf_op jit(solution)/shard_map/bij,bi->bj/dot_general | solution.py:61
  157.7 3.4 %all-to-all-start.3 = ((f32[8,27,128]{2,1,0:T(8,128)}), f32[8,27,128]{2,1,0:T(8,128)S(1)}, u32[]{:S(2)}, u32[]{:S(2)}) async-start(f32[8,27,128]{2,1,0:T(8,128)} %reshape.46), calls=%async_computation.5 | async-start | bytes 262144 | tf_op jit(solution)/shard_map/all_to_all | solution.py:63
  162.0 4.6 %all-to-all-done.3 = f32[8,27,128]{2,1,0:T(8,128)S(1)} async-done(((f32[8,27,128]{2,1,0:T(8,128)}), f32[8,27,128]{2,1,0:T(8,128)S(1)}, u32[]{:S(2)}, u32[]{:S(2)}) %all-to-all-start.3) | async-done | bytes 110624 | tf_op jit(solution)/shard_map/all_to_all | solution.py:63
  167.4 8.3 %all_gather.46 = f32[512,128]{1,0:T(8,128)S(1)} all-gather(f32[64,128]{1,0:T(8,128)S(1)} %get-tuple-element.13), channel_id=1, replica_groups=mesh['rows'=8,'hub'=4] {'rows'}, dimensions={0}, use_global_device_ids=true | all-gather | bytes 294912 | tf_op jit(solution)/shard_map/all_gather | solution.py:91
  176.3 9.2 %fusion.62 = f32[72,1,128]{2,1,0:T(1,128)S(1)} fusion(f32[72,128,1]{1,2,0:T(1,128)S(1)} %bitcast.114, f32[72,128,128]{2,1,0:T(8,128)} %param.15), kind=kOutput, calls=%fused_computation.109 | convolution fusion | flops 14155776 | bytes 4792320 | tf_op jit(solution)/shard_map/bij,bj->bi/dot_general | solution.py:93
  185.6 9.2 %all-gather.2 = f32[256,128]{1,0:T(8,128)S(1)} all-gather(f32[32,128]{1,0:T(8,128)} %reduce-scatter.8.cloned.1.call-done), channel_id=4, replica_groups=mesh['rows'=8,'hub'=4] {'rows'}, dimensions={0}, use_global_device_ids=true | all-gather | bytes 147456 | tf_op jit(solution)/shard_map/all_gather | solution.py:85
  195.5 13.1 %all_gather.47 = f32[128,128]{1,0:T(8,128)S(1)} all-gather(f32[32,128]{1,0:T(8,128)S(1)} %get-tuple-element.3), channel_id=1, replica_groups=mesh['rows'=8,'hub'=4] {'hub'}, dimensions={0}, use_global_device_ids=true | all-gather | bytes 81920 | tf_op jit(solution)/shard_map/all_gather | solution.py:90
  209.1 2.5 %fusion.63 = f32[24,1,128]{2,1,0:T(1,128)S(1)} fusion(f32[24,128,1]{1,2,0:T(1,128)S(1)} %bitcast.122, f32[24,128,128]{2,1,0:T(8,128)S(1)} %copy-done), kind=kOutput, calls=%fused_computation.110 | convolution fusion | flops 4718592 | bytes 1597440 | tf_op jit(solution)/shard_map/bij,bj->bi/dot_general | solution.py:94
  (94 shorter events, 34.2 us)
Async XLA Ops:
  7.2 11.3 %copy-start = (f32[24,128,128]{2,1,0:T(8,128)S(1)}, f32[24,128,128]{2,1,0:T(8,128)}, u32[]{:S(2)}) copy-start(f32[24,128,128]{2,1,0:T(8,128)} %param.19) | copy-start | bytes 4718596
  7.2 34.5 %copy-start.7 = (f32[64,128]{1,0:T(8,128)S(1)}, f32[64,128]{1,0:T(8,128)}, u32[]{:S(2)}) copy-start(f32[64,128]{1,0:T(8,128)} %param.22) | copy-start | bytes 98308
  7.2 34.5 %copy-start.3 = (f32[64,128]{1,0:T(8,128)S(1)}, f32[64,128]{1,0:T(8,128)}, u32[]{:S(2)}) copy-start(f32[64,128]{1,0:T(8,128)} %param.23) | copy-start | bytes 98308
  7.2 34.5 %copy-start.2 = (f32[64,128]{1,0:T(8,128)S(1)}, f32[64,128]{1,0:T(8,128)}, u32[]{:S(2)}) copy-start(f32[64,128]{1,0:T(8,128)} %param.24) | copy-start | bytes 98308
  11.3 20.7 %all-to-all-start = ((s32[8,1,27]{2,1,0:T(1,128)}), s32[8,1,27]{2,1,0:T(1,128)S(1)}, u32[]{:S(2)}, u32[]{:S(2)}) async-start(s32[8,1,27]{2,1,0:T(1,128)} %all_to_all.15), calls=%async_computation | async-start | bytes 8192 | tf_op jit(solution)/shard_map/all_to_all | solution.py:43
  16.5 43.7 %reduce-scatter.4.cloned.1.call-start = ((), (), s32[]{:S(2)}) async-start(), calls=%async_computation.7 | async-start | bytes 81920 | tf_op jit(solution)/shard_map/reduce_scatter | solution.py:84
  24.7 35.4 %copy-start.10 = (s32[72]{0:T(128)S(1)}, s32[72]{0:T(128)}, u32[]{:S(2)}) copy-start(s32[72]{0:T(128)} %param.16) | copy-start | bytes 868
  24.7 44.7 %copy-start.4 = (f32[32,128]{1,0:T(8,128)S(1)}, f32[32,128]{1,0:T(8,128)}, u32[]{:S(2)}) copy-start(f32[32,128]{1,0:T(8,128)} %param.27) | copy-start | bytes 49156
  24.7 44.7 %copy-start.5 = (f32[32,128]{1,0:T(8,128)S(1)}, f32[32,128]{1,0:T(8,128)}, u32[]{:S(2)}) copy-start(f32[32,128]{1,0:T(8,128)} %param.26) | copy-start | bytes 49156
  24.7 44.7 %copy-start.8 = (f32[32,128]{1,0:T(8,128)S(1)}, f32[32,128]{1,0:T(8,128)}, u32[]{:S(2)}) copy-start(f32[32,128]{1,0:T(8,128)} %param.25) | copy-start | bytes 49156
  30.5 55.6 %copy-start.1 = (f32[16,128]{1,0:T(8,128)S(1)}, f32[16,128]{1,0:T(8,128)}, u32[]{:S(2)}) copy-start(f32[16,128]{1,0:T(8,128)} %param.28) | copy-start | bytes 24580
  30.5 55.6 %copy-start.6 = (f32[16,128]{1,0:T(8,128)S(1)}, f32[16,128]{1,0:T(8,128)}, u32[]{:S(2)}) copy-start(f32[16,128]{1,0:T(8,128)} %param.29) | copy-start | bytes 24580
  30.5 55.6 %copy-start.11 = (s32[24]{0:T(128)S(1)}, s32[24]{0:T(128)}, u32[]{:S(2)}) copy-start(s32[24]{0:T(128)} %param.20) | copy-start | bytes 292
  32.0 9.7 %all-to-all-start.1 = ((f32[8,27,128]{2,1,0:T(8,128)}), f32[8,27,128]{2,1,0:T(8,128)S(1)}, u32[]{:S(2)}, u32[]{:S(2)}) async-start(f32[8,27,128]{2,1,0:T(8,128)} %reshape.42), calls=%async_computation.1 | async-start | bytes 262144 | tf_op jit(solution)/shard_map/all_to_all | solution.py:63
  69.4 30.1 %copy-start.9 = (s32[24]{0:T(128)S(1)}, s32[24]{0:T(128)}, u32[]{:S(2)}) copy-start(s32[24]{0:T(128)} %param.21) | copy-start | bytes 292
  94.6 8.8 %all-to-all-start.2 = ((f32[8,27,128]{2,1,0:T(8,128)}), f32[8,27,128]{2,1,0:T(8,128)S(1)}, u32[]{:S(2)}, u32[]{:S(2)}) async-start(f32[8,27,128]{2,1,0:T(8,128)} %reshape.44), calls=%async_computation.3 | async-start | bytes 262144 | tf_op jit(solution)/shard_map/all_to_all | solution.py:63
  98.0 23.9 %reduce-scatter.6.cloned.1.call-start = ((), (), s32[]{:S(2)}) async-start(), calls=%async_computation.8 | async-start | bytes 81920 | tf_op jit(solution)/shard_map/reduce_scatter | solution.py:84
  157.7 8.8 %all-to-all-start.3 = ((f32[8,27,128]{2,1,0:T(8,128)}), f32[8,27,128]{2,1,0:T(8,128)S(1)}, u32[]{:S(2)}, u32[]{:S(2)}) async-start(f32[8,27,128]{2,1,0:T(8,128)} %reshape.46), calls=%async_computation.5 | async-start | bytes 262144 | tf_op jit(solution)/shard_map/all_to_all | solution.py:63
  161.1 24.5 %reduce-scatter.8.cloned.1.call-start = ((), (), s32[]{:S(2)}) async-start(), calls=%async_computation.9 | async-start | bytes 81920 | tf_op jit(solution)/shard_map/reduce_scatter | solution.py:84
Sparse Core Ops, SparseCore 0:
  21.5 20.9 reduce-scatter.3
  101.1 20.6 reduce-scatter.5
  164.2 20.6 reduce-scatter.7
